TPU v7x, 32 devices: a whole 2x2x4 slice. The times are simulated.
32 devices in a mesh: dp: 4 (over y, core), vocab: 8 (over z, x).
Axes of the slice: x: 2, y: 2, z: 4, core: 2. Of those that a mesh axis runs over, the one named last changes fastest.
Arguments:
- latent_activations: bfloat16 [8, 448, 3584], P('dp', 'vocab'), as said below
- drawn_token_ids: int32 [8, 448], replicated, may hold values from 0 to 19455
- retained_ranking: int32 [4, 2], replicated, may hold values from 0 to 1, each once within a row
- unembedding_matrix: bfloat16 [3584, 19456], P('dp', 'vocab')
Outputs:
- logprob: float32 [4, 448], P('dp', 'vocab')
Inputs may be any that keep to these rules, and one draw needn't show every extreme that they name: `retained_ranking`: each row is an ordering of the 2 candidates of one data group; its first 1 entries are the surviving sequences. `latent_activations`: final hidden states.
All inputs are finite; a program needn't handle non-finite values.
Results may differ from a plain program's by a relative error of at most 0.0003.
Values may be sent and summed in bfloat16 or wider, within the bound.
A program may use at most 128 MiB of HBM per device.

v0:
```python
import jax
import jax.numpy as jnp
from jax import lax
from jax.sharding import PartitionSpec as P

RETAINED_SAMPLES = 1
BATCH_PROPOSALS = 2


def token_stats(logits, local_ids):
    highest = jnp.max(logits, axis=1)
    totals = jnp.sum(jnp.exp(logits - highest[:, None]), axis=1)
    columns = lax.broadcasted_iota(jnp.int32, logits.shape, 1)
    picked = jnp.sum(jnp.where(columns == local_ids[:, None], logits, 0.0), axis=1)
    return (highest, totals, picked)


def reduce_over(partials, reduce_axes):
    highest = jnp.max(partials[0], axis=reduce_axes)
    totals = jnp.sum(
        partials[1] * jnp.exp(partials[0] - jnp.expand_dims(highest, reduce_axes)), axis=reduce_axes
    )
    return (highest, totals, jnp.sum(partials[2], axis=reduce_axes))


def per_device(latent_activations, drawn_token_ids, retained_ranking, unembedding_matrix):
    n_vocab = lax.axis_size("vocab")
    n_data = lax.axis_size("dp")
    head_width = unembedding_matrix.shape[1]
    model_width = latent_activations.shape[2]
    per_dev = latent_activations.shape[1]
    vocab_index = lax.axis_index("vocab")
    cluster_number = lax.axis_index("dp")
    cluster_permutation = lax.dynamic_index_in_dim(
        retained_ranking, cluster_number, 0, keepdims=False
    )[:RETAINED_SAMPLES]
    survived = latent_activations[cluster_permutation]
    sub_width = head_width // n_data
    columns_here = lax.all_to_all(unembedding_matrix, "dp", split_axis=1, concat_axis=0, tiled=True)
    first_col = vocab_index * head_width + cluster_number * sub_width
    cluster_first_sample = jnp.arange(n_data, dtype=jnp.int32)[:, None] * BATCH_PROPOSALS
    complete_sample_array = (retained_ranking[:, :RETAINED_SAMPLES] + cluster_first_sample).reshape(
        -1
    )
    all_ids = drawn_token_ids[complete_sample_array].reshape(
        n_data, RETAINED_SAMPLES, n_vocab, per_dev
    )
    all_ids = all_ids.transpose(0, 2, 1, 3).reshape(n_data * n_vocab, RETAINED_SAMPLES, per_dev)
    shards = lax.all_gather(survived[None], ("dp", "vocab"), axis=0, tiled=True)
    row_count = shards.shape[0]
    block_logits = jnp.dot(
        shards.reshape(-1, model_width), columns_here, preferred_element_type=jnp.float32
    )
    block_ids = all_ids.reshape(-1)
    fresh = token_stats(block_logits, block_ids - first_col)
    partials = tuple((update.reshape(row_count, RETAINED_SAMPLES, per_dev) for update in fresh))
    partials = tuple(
        (item.reshape(n_data, n_vocab, RETAINED_SAMPLES, per_dev) for item in partials)
    )
    received = lax.all_to_all(
        lax.all_to_all(partials, "dp", split_axis=0, concat_axis=0, tiled=True),
        "vocab",
        split_axis=1,
        concat_axis=1,
        tiled=True,
    )
    result = reduce_over(received, (0, 1))
    return result[2] - (result[0] + jnp.log(result[1]))


def solution(mesh):
    return jax.shard_map(
        per_device,
        mesh=mesh,
        in_specs=(P("dp", "vocab", None), P(), P(), P("dp", "vocab")),
        out_specs=P("dp", "vocab"),
        check_vma=False,
    )
```

profile of v0, /device:TPU:0, one launch (start us, length us, event | category | flops | bytes accessed | tf_op | source)
XLA Modules:
  0.0 199.0 jit_solution(13328502885842392912)
XLA Ops:
  6.5 0.0 copy-start
  6.5 0.0 all-gather.3.cloned.1.call-start
  6.5 0.8 constant_dynamic-slice_fusion.1
  7.4 0.5 slice.10
  9.8 0.0 copy-done
  9.8 0.8 constant_dynamic-slice_fusion
  10.6 0.0 all-gather.3.cloned.1.call-update
  10.6 7.1 %copy.14 = bf16[896,2432]{0,1:T(8,128)(2,1)} copy(bf16[896,2432]{1,0:T(8,128)(2,1)} %param.7) | data formatting | bytes 8716288 | tf_op args[3]
  17.7 0.0 copy-start.2
  17.7 0.0 copy-start.1
  17.7 5.0 %all-to-all-start = ((bf16[896,4,608]{0,2,1:T(8,128)(2,1)}), bf16[896,4,608]{0,2,1:T(8,128)(2,1)}, u32[]{:S(2)}, u32[]{:S(2)}) async-start(bf16[896,4,608]{0,2,1:T(8,128)(2,1)} %bitcast.43), calls=%async_computation | async-start | bytes 8716288 | tf_op jit(solution)/shard_map/all_to_all | solution.py:39
  22.8 0.0 copy-done.2
  22.8 0.0 copy-done.1
  22.8 0.6 gather_fusion
  23.4 0.1 sub.45
  23.5 65.6 %all-to-all-done = bf16[896,4,608]{0,2,1:T(8,128)(2,1)} async-done(((bf16[896,4,608]{0,2,1:T(8,128)(2,1)}), bf16[896,4,608]{0,2,1:T(8,128)(2,1)}, u32[]{:S(2)}, u32[]{:S(2)}) %all-to-all-start) | async-done | bytes 4358176 | tf_op jit(solution)/shard_map/all_to_all | solution.py:39
  89.1 7.2 %copy.15 = bf16[4,896,608]{2,1,0:T(8,128)(2,1)} copy(bf16[4,896,608]{1,2,0:T(8,128)(2,1)} %bitcast.5) | data formatting | bytes 8716288 | tf_op jit(solution)/shard_map/all_to_all | solution.py:39
  96.3 24.2 %all-gather.3.cloned.1.call-done = bf16[32,56,3584]{2,1,0:T(8,128)(2,1)} async-done(((bf16[1,56,3584]{2,1,0:T(8,128)(2,1)}), bf16[32,56,3584]{2,1,0:T(8,128)(2,1)}) %all-gather.3.cloned.1.call-update) | async-done | bytes 12845072 | tf_op jit(solution)/shard_map/all_gather | solution.py:49
  120.5 15.0 %fusion.1 = (f32[1792]{0:T(1024)S(1)}, f32[1792,608]{0,1:T(8,128)}) fusion(bf16[1792,3584]{1,0:T(8,128)(2,1)} %bitcast.51, bf16[3584,608]{1,0:T(8,128)(2,1)} %bitcast.44), kind=kOutput, calls=%fused_computation.12 | convolution fusion | flops 7810881536 | bytes 21568512 | tf_op jit(solution)/shard_map/dot_general | solution.py:51
  135.6 0.1 reshape_reshape.10
  135.6 3.4 %exponential_reduce_fusion = (f32[1792]{0:T(1024)S(1)}, f32[1792]{0:T(1024)S(1)}) fusion(f32[1792,608]{0,1:T(8,128)} %get-tuple-element.19, f32[1792]{0:T(1024)S(1)} %get-tuple-element.18, s32[1792]{0:T(1024)S(1)} %sub.45), kind=kLoop, calls=%fused_computation.1 | loop fusion | flops 5444096 | bytes 4386816 | tf_op jit(solution)/shard_map/reduce_sum | solution.py:12
  139.0 0.1 reshape_reshape.11
  139.1 0.7 reshape.99
  139.8 3.2 %all-to-all-start.5 = ((f32[4,1,448]{2,1,0:T(1,128)}), f32[4,1,448]{2,1,0:T(1,128)S(1)}, u32[]{:S(2)}, u32[]{:S(2)}) async-start(f32[4,1,448]{2,1,0:T(1,128)} %reshape.99), calls=%async_computation.5 | async-start | bytes 16384 | tf_op jit(solution)/shard_map/all_to_all | solution.py:61
  143.1 0.7 reshape.95
  143.7 0.1 reshape_reshape.9
  143.8 3.0 %all-to-all-done.5 = f32[4,1,448]{2,1,0:T(1,128)S(1)} async-done(((f32[4,1,448]{2,1,0:T(1,128)}), f32[4,1,448]{2,1,0:T(1,128)S(1)}, u32[]{:S(2)}, u32[]{:S(2)}) %all-to-all-start.5) | async-done | bytes 7200 | tf_op jit(solution)/shard_map/all_to_all | solution.py:61
  146.8 3.2 %all-to-all-start.3 = ((f32[4,1,448]{2,1,0:T(1,128)}), f32[4,1,448]{2,1,0:T(1,128)S(1)}, u32[]{:S(2)}, u32[]{:S(2)}) async-start(f32[4,1,448]{2,1,0:T(1,128)} %reshape.95), calls=%async_computation.3 | async-start | bytes 16384 | tf_op jit(solution)/shard_map/all_to_all | solution.py:61
  150.1 0.7 reshape.91
  150.8 3.1 %all-to-all-done.3 = f32[4,1,448]{2,1,0:T(1,128)S(1)} async-done(((f32[4,1,448]{2,1,0:T(1,128)}), f32[4,1,448]{2,1,0:T(1,128)S(1)}, u32[]{:S(2)}, u32[]{:S(2)}) %all-to-all-start.3) | async-done | bytes 7200 | tf_op jit(solution)/shard_map/all_to_all | solution.py:61
  153.9 3.2 %all-to-all-start.1 = ((f32[4,1,448]{2,1,0:T(1,128)}), f32[4,1,448]{2,1,0:T(1,128)S(1)}, u32[]{:S(2)}, u32[]{:S(2)}) async-start(f32[4,1,448]{2,1,0:T(1,128)} %reshape.91), calls=%async_computation.1 | async-start | bytes 16384 | tf_op jit(solution)/shard_map/all_to_all | solution.py:61
  157.1 0.5 broadcast.53
  157.6 0.7 reduce.6
  158.3 0.1 reshape.96
  158.4 0.7 reduce.7
  159.1 0.7 reshape.97
  159.8 1.1 all-to-all-done.1
  160.9 3.8 %all-to-all-start.4 = ((f32[8,1,224]{2,1,0:T(1,128)}), f32[8,1,224]{2,1,0:T(1,128)S(1)}, u32[]{:S(2)}, u32[]{:S(2)}) async-start(f32[8,1,224]{2,1,0:T(1,128)} %reshape.97), calls=%async_computation.4 | async-start | bytes 16384 | tf_op jit(solution)/shard_map/all_to_all | solution.py:60
  164.7 0.7 reduce.9
  165.3 0.1 reshape.100
  165.4 0.7 reduce.10
  166.2 0.7 reshape.101
  166.8 4.3 %all-to-all-done.4 = f32[8,1,224]{2,1,0:T(1,128)S(1)} async-done(((f32[8,1,224]{2,1,0:T(1,128)}), f32[8,1,224]{2,1,0:T(1,128)S(1)}, u32[]{:S(2)}, u32[]{:S(2)}) %all-to-all-start.4) | async-done | bytes 7200 | tf_op jit(solution)/shard_map/all_to_all | solution.py:60
  171.2 3.3 %all-to-all-start.6 = ((f32[8,1,224]{2,1,0:T(1,128)}), f32[8,1,224]{2,1,0:T(1,128)S(1)}, u32[]{:S(2)}, u32[]{:S(2)}) async-start(f32[8,1,224]{2,1,0:T(1,128)} %reshape.101), calls=%async_computation.6 | async-start | bytes 16384 | tf_op jit(solution)/shard_map/all_to_all | solution.py:60
  174.5 0.7 reduce.3
  175.2 0.1 reshape.92
  175.3 0.7 reduce.4
  176.0 0.7 reshape.93
  176.7 0.7 reduce.8
  177.4 0.1 reshape.98
  177.5 3.5 %all-to-all-done.6 = f32[8,1,224]{2,1,0:T(1,128)S(1)} async-done(((f32[8,1,224]{2,1,0:T(1,128)}), f32[8,1,224]{2,1,0:T(1,128)S(1)}, u32[]{:S(2)}, u32[]{:S(2)}) %all-to-all-start.6) | async-done | bytes 7200 | tf_op jit(solution)/shard_map/all_to_all | solution.py:60
  181.0 3.3 %all-to-all-start.2 = ((f32[8,1,224]{2,1,0:T(1,128)}), f32[8,1,224]{2,1,0:T(1,128)S(1)}, u32[]{:S(2)}, u32[]{:S(2)}) async-start(f32[8,1,224]{2,1,0:T(1,128)} %reshape.93), calls=%async_computation.2 | async-start | bytes 16384 | tf_op jit(solution)/shard_map/all_to_all | solution.py:60
  184.3 0.1 bitcast_reduce_fusion
  184.4 0.7 reduce.11
  185.0 0.1 reshape.102
  185.1 5.6 %all-to-all-done.2 = f32[8,1,224]{2,1,0:T(1,128)S(1)} async-done(((f32[8,1,224]{2,1,0:T(1,128)}), f32[8,1,224]{2,1,0:T(1,128)S(1)}, u32[]{:S(2)}, u32[]{:S(2)}) %all-to-all-start.2) | async-done | bytes 7200 | tf_op jit(solution)/shard_map/all_to_all | solution.py:60
  190.8 0.7 reduce.5
  191.4 0.1 reshape.94
  191.5 0.1 bitcast_reduce_fusion.1
  191.6 0.1 multiply_reduce_fusion
  191.6 0.5 subtract_bitcast_fusion
  (9 shorter events, 0.1 us)
Async XLA Ops:
  6.5 3.3 %copy-start = (bf16[2,56,3584]{2,1,0:T(8,128)(2,1)S(1)}, bf16[2,56,3584]{2,1,0:T(8,128)(2,1)}, u32[]{:S(2)}) copy-start(bf16[2,56,3584]{2,1,0:T(8,128)(2,1)} %param.4) | copy-start | bytes 2408452
  6.5 114.0 %all-gather.3.cloned.1.call-start = ((), (), s32[]{:S(2)}) async-start(), calls=%async_computation.7 | async-start | bytes 13246464 | tf_op jit(solution)/shard_map/all_gather | solution.py:49
  17.7 5.1 %copy-start.2 = (s32[4,2]{0,1:T(2,128)S(1)}, s32[4,2]{0,1:T(2,128)}, u32[]{:S(2)}) copy-start(s32[4,2]{0,1:T(2,128)} %param.6) | copy-start | bytes 100
  17.7 5.1 %copy-start.1 = (s32[8,448]{1,0:T(8,128)S(1)}, s32[8,448]{1,0:T(8,128)}, u32[]{:S(2)}) copy-start(s32[8,448]{1,0:T(8,128)} %param.5) | copy-start | bytes 43012
  17.7 71.3 %all-to-all-start = ((bf16[896,4,608]{0,2,1:T(8,128)(2,1)}), bf16[896,4,608]{0,2,1:T(8,128)(2,1)}, u32[]{:S(2)}, u32[]{:S(2)}) async-start(bf16[896,4,608]{0,2,1:T(8,128)(2,1)} %bitcast.43), calls=%async_computation | async-start | bytes 8716288 | tf_op jit(solution)/shard_map/all_to_all | solution.py:39
  139.8 7.0 %all-to-all-start.5 = ((f32[4,1,448]{2,1,0:T(1,128)}), f32[4,1,448]{2,1,0:T(1,128)S(1)}, u32[]{:S(2)}, u32[]{:S(2)}) async-start(f32[4,1,448]{2,1,0:T(1,128)} %reshape.99), calls=%async_computation.5 | async-start | bytes 16384 | tf_op jit(solution)/shard_map/all_to_all | solution.py:61
  146.8 7.0 %all-to-all-start.3 = ((f32[4,1,448]{2,1,0:T(1,128)}), f32[4,1,448]{2,1,0:T(1,128)S(1)}, u32[]{:S(2)}, u32[]{:S(2)}) async-start(f32[4,1,448]{2,1,0:T(1,128)} %reshape.95), calls=%async_computation.3 | async-start | bytes 16384 | tf_op jit(solution)/shard_map/all_to_all | solution.py:61
  153.9 7.0 %all-to-all-start.1 = ((f32[4,1,448]{2,1,0:T(1,128)}), f32[4,1,448]{2,1,0:T(1,128)S(1)}, u32[]{:S(2)}, u32[]{:S(2)}) async-start(f32[4,1,448]{2,1,0:T(1,128)} %reshape.91), calls=%async_computation.1 | async-start | bytes 16384 | tf_op jit(solution)/shard_map/all_to_all | solution.py:61
  160.9 10.3 %all-to-all-start.4 = ((f32[8,1,224]{2,1,0:T(1,128)}), f32[8,1,224]{2,1,0:T(1,128)S(1)}, u32[]{:S(2)}, u32[]{:S(2)}) async-start(f32[8,1,224]{2,1,0:T(1,128)} %reshape.97), calls=%async_computation.4 | async-start | bytes 16384 | tf_op jit(solution)/shard_map/all_to_all | solution.py:60
  171.2 9.8 %all-to-all-start.6 = ((f32[8,1,224]{2,1,0:T(1,128)}), f32[8,1,224]{2,1,0:T(1,128)S(1)}, u32[]{:S(2)}, u32[]{:S(2)}) async-start(f32[8,1,224]{2,1,0:T(1,128)} %reshape.101), calls=%async_computation.6 | async-start | bytes 16384 | tf_op jit(solution)/shard_map/all_to_all | solution.py:60
  181.0 9.8 %all-to-all-start.2 = ((f32[8,1,224]{2,1,0:T(1,128)}), f32[8,1,224]{2,1,0:T(1,128)S(1)}, u32[]{:S(2)}, u32[]{:S(2)}) async-start(f32[8,1,224]{2,1,0:T(1,128)} %reshape.93), calls=%async_computation.2 | async-start | bytes 16384 | tf_op jit(solution)/shard_map/all_to_all | solution.py:60
Sparse Core Ops, SparseCore 0:
  10.8 109.7 all-gather.2
where the time goes:
time: 200 us; the launch traced here: 199 us
  waiting for transfers between devices  111 us (56%)
  starting transfers between devices  25.2 us (13%)
  local copies, waits for them, and re-layouts  22.5 us (11%)
  between operations  15.6 us (8%)
  matrix products  15 us (8%)
  other arithmetic  10.2 us (5%)
    all_to_all x1, waiting for transfers between devices, per_device(): lax.all_to_all(unembedding_matrix, 'dp', split_axis=1, concat_axis=0, til...  65.6 us
    all_gather x1, waiting for transfers between devices, per_device(): shards = lax.all_gather(survived[None], ('dp', 'vocab'), axis=0, tiled=True)  24.2 us
    dot_general x1, matrix products, per_device(): jnp.dot(shards.reshape(-1, model_width), columns_here, preferred_element_...  15 us
    all_to_all x3, waiting for transfers between devices, per_device(): lax.all_to_all(lax.all_to_all(partials, 'dp', split_axis=0, concat_axis=0...  13.5 us
    unnamed x22, local copies, waits for them, and re-layouts  11.7 us
    all_to_all x3, starting transfers between devices, per_device(): lax.all_to_all(lax.all_to_all(partials, 'dp', split_axis=0, concat_axis=0...  10.4 us
    all_to_all x3, starting transfers between devices, per_device(): lax.all_to_all(partials, 'dp', split_axis=0, concat_axis=0, tiled=True)  9.73 us
    all_to_all x1, local copies, waits for them, and re-layouts, per_device(): lax.all_to_all(unembedding_matrix, 'dp', split_axis=1, concat_axis=0, til...  7.21 us
  transfers between devices with their start and end apart: 8, of which 8 were waited for; matrix products, arithmetic and copies ran while one was open for 13% of the time, Pallas kernels for 0%

commit v1 on v0

v1 whole, which is shorter than its diff:
```python
import functools
import math

import jax
import jax.numpy as jnp
from jax import lax
from jax.experimental import pallas as pl
from jax.experimental.pallas import tpu as pltpu
from jax.sharding import PartitionSpec as P

BATCH_PROPOSALS = 2
MESH = pl.DeviceIdType.MESH
LANES = 128


class Plan:
    def __init__(self, n_dp, n_vocab, per_dev, width, depth):
        self.ny = n_dp // 2
        nx = math.isqrt(max(n_vocab // 2, 1))
        while n_vocab % nx:
            nx -= 1
        self.nx, self.nz = nx, n_vocab // nx
        self.n_dp, self.n_vocab = n_dp, n_vocab
        self.chips = self.ny * n_vocab
        self.per_dev = per_dev
        rows = 16
        while rows < per_dev:
            rows *= 2
        self.rows = rows
        self.tokens = self.chips * rows
        self.depth = depth
        tiles = width // LANES
        self.tiles = tiles
        self.own_tiles = -(-tiles // self.ny)
        self.cw = 2 * LANES if self.own_tiles % 2 == 0 else LANES
        self.cols = self.own_tiles * LANES
        self.chunks = self.cols // self.cw
        self.m_tile = min(512, self.tokens)

    def start(self, y):
        return jnp.minimum(y * self.own_tiles, self.tiles - self.own_tiles) * LANES


def flow_items(plan, order, flip):
    sizes = {"y": plan.ny, "x": plan.nx, "z": plan.nz}
    reach = {}
    for axis, n in sizes.items():
        far, near = n // 2, (n - 1) // 2
        reach[axis] = (near, far) if flip and axis == "z" else (far, near)
    items = []

    def visit(offset, last):
        sends = []
        for place, axis in enumerate(order):
            if place < last:
                continue
            plus, minus = reach[axis]
            at = offset.get(axis, 0)
            if at >= 0 and at < plus:
                sends.append((axis, 1))
            if at <= 0 and -at < minus:
                sends.append((axis, -1))
        items.append((dict(offset), sends))
        for axis, step in sends:
            moved = dict(offset)
            moved[axis] = moved.get(axis, 0) + step
            visit(moved, order.index(axis))

    visit({}, 0)
    items.sort(key=lambda item: sum(abs(v) for v in item[0].values()))
    return items


def kernel(plan, rank_ref, lat_ref, ids_ref, w_ref, out_ref, xbuf, wbuf, lg, m_ref, s_ref, p_ref, stats, got,
           x_send, x_recv, wl_sem, wy_send, wy_recv, wp_send, wp_recv, st_send, st_recv):
    ny, nx, nz, chips, rows = plan.ny, plan.nx, plan.nz, plan.chips, plan.rows
    dp, vocab = lax.axis_index("dp"), lax.axis_index("vocab")
    y, core = dp // 2, dp % 2
    z, x = vocab // nx, vocab % nx
    me = vocab * ny + y
    half = lat_ref.shape[2] // 2
    depth, cw = plan.depth, plan.cw

    def chip_device(b):
        return {"dp": (b % ny) * 2 + core, "vocab": b // ny}

    partner = {"dp": y * 2 + (1 - core), "vocab": vocab}

    base = pl.multiple_of(me * rows, rows)
    if rows != plan.per_dev:
        xbuf[pl.ds(base, rows), :] = jnp.zeros((rows, 2 * half), jnp.bfloat16)
    xbuf[pl.ds(base, plan.per_dev), :] = lat_ref[rank_ref[dp, 0]]

    barrier = pltpu.get_barrier_semaphore()

    @pl.loop(1, chips)
    def _(k):
        pl.semaphore_signal(barrier, inc=1, device_id=chip_device((me + k) % chips), device_id_type=MESH)

    pl.semaphore_signal(barrier, inc=1, device_id=partner, device_id_type=MESH)

    def w_rows(d):
        return pl.ds(pl.multiple_of(d * depth, depth), depth)

    def w_cols(j):
        return pl.ds(j * cw, cw)

    def window(y_at, j):
        return pl.ds(pl.multiple_of(plan.start(y_at) + j * cw, LANES), cw)

    locals_ = [
        pltpu.make_async_copy(w_ref.at[:, window(y, j)], wbuf.at[w_rows(dp), w_cols(j)], wl_sem.at[j])
        for j in range(plan.chunks)
    ]
    for copy in locals_:
        copy.start()
    pl.semaphore_wait(barrier, chips)

    def x_slice(flow, b):
        return xbuf.at[pl.ds(pl.multiple_of(b * rows, rows), rows), pl.ds(flow * half, half)]

    def origin(offset):
        oy = lax.rem(y - offset.get("y", 0) + ny, ny)
        ox = lax.rem(x - offset.get("x", 0) + nx, nx)
        oz = lax.rem(z - offset.get("z", 0) + nz, nz)
        return (oz * nx + ox) * ny + oy

    def x_copy(flow, b, axis, step):
        ty = lax.rem(y + (step if axis == "y" else 0) + ny, ny)
        tx = lax.rem(x + (step if axis == "x" else 0) + nx, nx)
        tz = lax.rem(z + (step if axis == "z" else 0) + nz, nz)
        return pltpu.make_async_remote_copy(
            src_ref=x_slice(flow, b), dst_ref=x_slice(flow, b), send_sem=x_send, recv_sem=x_recv.at[flow, b],
            device_id={"dp": ty * 2 + core, "vocab": tz * nx + tx}, device_id_type=MESH,
        )

    flows = (flow_items(plan, ("y", "x", "z"), False), flow_items(plan, ("y", "z", "x"), True))

    def wy_copy(k, j):
        y_to = lax.rem(y + k, ny)
        return pltpu.make_async_remote_copy(
            src_ref=w_ref.at[:, window(y_to, j)], dst_ref=wbuf.at[w_rows(dp), w_cols(j)],
            send_sem=wy_send.at[k, j], recv_sem=wy_recv.at[k, j],
            device_id={"dp": y_to * 2 + core, "vocab": vocab}, device_id_type=MESH,
        )

    def wp_copy(k, j):
        d = lax.rem(y - k + ny, ny) * 2 + core
        place = wbuf.at[w_rows(d), w_cols(j)]
        return pltpu.make_async_remote_copy(
            src_ref=w_ref.at[:, window(y, j)] if k == 0 else place, dst_ref=place,
            send_sem=wp_send.at[k, j], recv_sem=wp_recv.at[k, j],
            device_id=partner, device_id_type=MESH,
        )

    started = []
    for flow in range(2):
        offset, sends = flows[flow][0]
        for axis, step in sends:
            x_copy(flow, me, axis, step).start()
    for j in range(plan.chunks):
        for k in range(1, ny):
            copy = wy_copy(k, j)
            copy.start()
            started.append(copy)
    for j in range(plan.chunks):
        copy = wp_copy(0, j)
        copy.start()
        started.append(copy)

    def forward_w(j):
        for k in range(1, ny):
            wy_copy(k, j).wait_recv()
            copy = wp_copy(k, j)
            copy.start()
            started.append(copy)

    todo = [(flow, item) for pair in zip(flows[0][1:], flows[1][1:]) for flow, item in enumerate(pair)]
    due = 0
    for count, (flow, (offset, sends)) in enumerate(todo):
        b = origin(offset)
        x_copy(flow, b, "y", 0).wait_recv()
        for axis, step in sends:
            x_copy(flow, b, axis, step).start()
        while due < plan.chunks - 1 and (count + 1) * (plan.chunks - 0.5) >= (due + 2) * len(todo):
            forward_w(due)
            due += 1

    m_ref[...] = jnp.full(m_ref.shape, -jnp.inf, jnp.float32)
    s_ref[...] = jnp.zeros(s_ref.shape, jnp.float32)
    p_ref[...] = jnp.zeros(p_ref.shape, jnp.float32)
    lane = lax.broadcasted_iota(jnp.int32, (1, LANES), 1)
    repeated = y * plan.own_tiles * LANES - plan.start(y)
    for j in range(plan.chunks):
        while due < min(plan.chunks, j + 1):
            forward_w(due)
            due += 1
        locals_[j].wait()
        for k in range(ny):
            wp_copy(k, j).wait_recv()

        @pl.loop(0, plan.tokens // plan.m_tile)
        def _(i, j=j):
            top = pl.multiple_of(i * plan.m_tile, plan.m_tile)
            lg[...] = jnp.dot(
                xbuf[pl.ds(top, plan.m_tile), :], wbuf[:, w_cols(j)], preferred_element_type=jnp.float32
            )

            @pl.loop(0, plan.m_tile // 32, unroll=2)
            def _(r):
                here = pl.ds(pl.multiple_of(r * 32, 32), 32)
                there = pl.ds(pl.multiple_of(top + r * 32, 32), 32)
                parts = [lg[here, pl.ds(c * LANES, LANES)] for c in range(cw // LANES)]
                before = m_ref[there, :]
                now = before
                for part in parts:
                    now = jnp.maximum(now, part)
                total = s_ref[there, :] * jnp.exp(before - now)
                picked = p_ref[there, :]
                ids = ids_ref[there, :]
                for c, part in enumerate(parts):
                    first = j * cw + c * LANES
                    columns = lane + first
                    term = jnp.exp(part - now)
                    match = columns == ids
                    if first < (plan.own_tiles * ny - plan.tiles) * LANES:
                        own = columns >= repeated
                        term = jnp.where(own, term, 0.0)
                        match = jnp.logical_and(match, own)
                    total = total + term
                    picked = picked + jnp.where(match, part, 0.0)
                m_ref[there, :] = now
                s_ref[there, :] = total
                p_ref[there, :] = picked

    for g in range(plan.tokens // LANES):
        here = pl.ds(g * LANES, LANES)
        m = m_ref[here, :]
        top = jnp.max(m, axis=1, keepdims=True)
        total = jnp.sum(s_ref[here, :] * jnp.exp(m - top), axis=1, keepdims=True)
        picked = jnp.sum(p_ref[here, :], axis=1, keepdims=True)
        both = jnp.where(lane == 0, top, jnp.where(lane == 1, total, picked))
        stats[g] = both.T[:8, :]

    per_group = LANES // rows

    def st_copy(k):
        b = lax.rem(me + k, chips)
        return pltpu.make_async_remote_copy(
            src_ref=stats.at[b // per_group], dst_ref=got.at[k], send_sem=st_send, recv_sem=st_recv,
            device_id=chip_device(b), device_id_type=MESH,
        )

    @pl.loop(1, chips)
    def _(k):
        st_copy(k).start()

    got[0] = stats[me // per_group]
    for copy in started:
        copy.wait_send()
    sent = xbuf.at[pl.ds(0, (chips - 1) * rows), :]
    pltpu.make_async_copy(sent, sent, x_send).wait()
    others = got.at[pl.ds(1, chips - 1)]
    pltpu.make_async_copy(others, others, st_send).wait()
    pltpu.make_async_copy(others, others, st_recv).wait()
    top = got[0][0:1, :]
    for b in range(1, chips):
        top = jnp.maximum(top, got[b][0:1, :])
    total = jnp.zeros_like(top)
    picked = jnp.zeros_like(top)
    for b in range(chips):
        total = total + got[b][1:2, :] * jnp.exp(got[b][0:1, :] - top)
        picked = picked + got[b][2:3, :]
    result = picked - (top + jnp.log(total))
    place = lax.rem(me, per_group)
    value = result[:, : plan.per_dev]
    for c in range(1, per_group):
        value = jnp.where(place == c, result[:, c * rows : c * rows + plan.per_dev], value)
    out_ref[...] = value


def per_device(latent_activations, drawn_token_ids, retained_ranking, unembedding_matrix):
    depth, width = unembedding_matrix.shape
    n_dp, n_vocab = lax.axis_size("dp"), lax.axis_size("vocab")
    per_dev = latent_activations.shape[1]
    plan = Plan(n_dp, n_vocab, per_dev, width, depth)
    dp, vocab = lax.axis_index("dp"), lax.axis_index("vocab")
    ids = drawn_token_ids.reshape(n_dp, BATCH_PROPOSALS, n_vocab * per_dev)
    ids = jnp.where(retained_ranking[:, :1] == 0, ids[:, 0], ids[:, 1])
    ids = ids.reshape(plan.ny, 2, n_vocab, per_dev)
    ids = jnp.where(dp % 2 == 0, ids[:, 0], ids[:, 1]).transpose(1, 0, 2)
    ids = ids - (vocab * width + plan.start(dp // 2))
    ids = jnp.pad(ids, ((0, 0), (0, 0), (0, plan.rows - per_dev)), constant_values=-1)
    ids = ids.reshape(plan.tokens, 1)
    dma, vmem = pltpu.SemaphoreType.DMA, pltpu.VMEM
    model = depth * n_dp
    return pl.pallas_call(
        functools.partial(kernel, plan),
        out_shape=jax.ShapeDtypeStruct((1, per_dev), jnp.float32),
        in_specs=[
            pl.BlockSpec(memory_space=pltpu.SMEM),
            pl.BlockSpec(memory_space=vmem),
            pl.BlockSpec(memory_space=vmem),
            pl.BlockSpec(memory_space=pl.ANY),
        ],
        out_specs=pl.BlockSpec(memory_space=vmem),
        scratch_shapes=[
            vmem((plan.tokens, model), jnp.bfloat16),
            vmem((model, plan.cols), jnp.bfloat16),
            vmem((plan.m_tile, plan.cw), jnp.float32),
            vmem((plan.tokens, LANES), jnp.float32),
            vmem((plan.tokens, LANES), jnp.float32),
            vmem((plan.tokens, LANES), jnp.float32),
            vmem((plan.tokens // LANES, 8, LANES), jnp.float32),
            vmem((plan.chips, 8, LANES), jnp.float32),
            dma, dma((2, plan.chips)),
            dma((plan.chunks,)),
            dma((plan.ny, plan.chunks)), dma((plan.ny, plan.chunks)),
            dma((plan.ny, plan.chunks)), dma((plan.ny, plan.chunks)),
            dma, dma,
        ],
        compiler_params=pltpu.CompilerParams(
            collective_id=0, has_side_effects=True, vmem_limit_bytes=56 * 2**20
        ),
        name="score",
    )(retained_ranking, latent_activations, ids, unembedding_matrix)


def solution(mesh):
    return jax.shard_map(
        per_device,
        mesh=mesh,
        in_specs=(P("dp", "vocab", None), P(), P(), P("dp", "vocab")),
        out_specs=P("dp", "vocab"),
        check_vma=False,
    )
```

time: 200 us -> 131 us (0.66)
  Pallas kernels: 0 us -> 125 us
  waiting for transfers between devices: 111 us -> 0 us
  starting transfers between devices: 25.2 us -> 0 us
  local copies, waits for them, and re-layouts: 22.5 us -> 4.76 us
  between operations: 15.6 us -> 0.03 us
  matrix products: 15 us -> 0 us
  other arithmetic: 10.2 us -> 0.79 us
    pallas_call x0 -> x1, Pallas kernels: none -> 125 us  [per_device(): pl.pallas_call(functools.partial(kernel, plan), out_shape=jax.ShapeDtypeS...]
    all_to_all x7 -> x0, waiting for transfers between devices: 86.3 us -> none  [the longest x1 65.6 us: per_device(): lax.all_to_all(unembedding_matrix, 'dp', split_axis=1, concat_axis=0, til...]
    all_to_all x7 -> x0, starting transfers between devices: 25.2 us -> none  [the longest x3 10.4 us: per_device(): lax.all_to_all(lax.all_to_all(partials, 'dp', split_axis=0, concat_axis=0...]
    all_gather x1 -> x0, waiting for transfers between devices: 24.2 us -> none  [per_device(): shards = lax.all_gather(survived[None], ('dp', 'vocab'), axis=0, tiled=True)]
    dot_general x1 -> x0, matrix products: 15 us -> none  [per_device(): jnp.dot(shards.reshape(-1, model_width), columns_here, preferred_element_...]
    unnamed x22 -> x5, local copies, waits for them, and re-layouts: 11.7 us -> 2.47 us
    all_to_all x5 -> x0, local copies, waits for them, and re-layouts: 7.78 us -> none  [the longest x1 7.21 us: per_device(): lax.all_to_all(unembedding_matrix, 'dp', split_axis=1, concat_axis=0, til...]
    all_to_all x6 -> x0, other arithmetic: 4.03 us -> none  [the longest x3 2.02 us: per_device(): lax.all_to_all(partials, 'dp', split_axis=0, concat_axis=0, tiled=True)]
  transfers between devices with their start and end apart: 8 -> 0, of which waited for: 8 -> 0; matrix products, arithmetic and copies ran while one was open for 13% -> 0% of each run, Pallas kernels for 0% -> 0%
where the time goes in v1:
time: 131 us; the launch traced here: 130 us
  Pallas kernels  125 us (95%)
  local copies, waits for them, and re-layouts  4.76 us (4%)
    pallas_call x1, Pallas kernels, per_device(): pl.pallas_call(functools.partial(kernel, plan), out_shape=jax.ShapeDtypeS...  125 us

profile of v1, /device:TPU:0, one launch (start us, length us, event | category | flops | bytes accessed | tf_op | source)
XLA Modules:
  0.0 130.3 jit_solution(1448703033218125146)
XLA Ops:
  0.0 0.7 reshape.18
  0.8 0.1 squeeze.8
  0.8 0.1 squeeze.9
  0.9 0.7 compare_reduce_fusion
  1.6 0.1 broadcast_in_dim.10
  1.7 0.1 broadcast_select_fusion
  1.8 1.3 reshape.20.ids_ref
  3.1 1.4 %copy.10.rank_ref = s32[4,2]{1,0:T(4,128)} copy(s32[4,2]{0,1:T(2,128)} %param.6) | data formatting | bytes 64 | tf_op args[2]
  4.5 124.7 %score.1 = f32[1,56]{1,0:T(1,128)} custom-call(s32[4,2]{1,0:T(4,128)} %copy.10.rank_ref, bf16[2,56,3584]{2,1,0:T(8,128)(2,1)} %lat_ref.1, s32[1024,1]{1,0:T(8,128)} %reshape.20.ids_ref, bf16[896,2432]{1,0:T(8,128)(2,1)} %w_ref.1), custom_call_target="tpu_custom_call" | custom-call | tf_op jit(solution)/shard_map/score/pallas_call | solution.py:297
  129.2 1.1 copy.16
  (6 shorter events, 0.0 us)

commit v2 on v1

--- a/solution.py
+++ b/solution.py
@@ -35,40 +35,28 @@
         self.cw = 2 * LANES if self.own_tiles % 2 == 0 else LANES
         self.cols = self.own_tiles * LANES
         self.chunks = self.cols // self.cw
-        self.m_tile = min(512, self.tokens)
+        self.m_tile = self.nx * self.ny * rows
+        self.sent_rows = per_dev if per_dev % 8 == 0 else rows
+
+    def x_sends(self):
+        ny, nx, nz = self.ny, self.nx, self.nz
+        fan = {n: min(n - 1, 2) for n in (ny, nx, nz)}
+        on = {n: int(n > 2) for n in (ny, nx, nz)}
+        count = 2 * (fan[ny] + fan[nx] + fan[nz]) + 2 * (ny - 1) * (on[ny] + fan[nx] + fan[nz])
+        count += (nx - 1) * ny * (on[nx] + fan[nz]) + (nz - 1) * nx * ny * on[nz]
+        return count + (nz - 1) * ny * (on[nz] + fan[nx]) + nz * (nx - 1) * ny * on[nx]
 
     def start(self, y):
         return jnp.minimum(y * self.own_tiles, self.tiles - self.own_tiles) * LANES
 
 
-def flow_items(plan, order, flip):
-    sizes = {"y": plan.ny, "x": plan.nx, "z": plan.nz}
-    reach = {}
-    for axis, n in sizes.items():
-        far, near = n // 2, (n - 1) // 2
-        reach[axis] = (near, far) if flip and axis == "z" else (far, near)
-    items = []
-
-    def visit(offset, last):
-        sends = []
-        for place, axis in enumerate(order):
-            if place < last:
-                continue
-            plus, minus = reach[axis]
-            at = offset.get(axis, 0)
-            if at >= 0 and at < plus:
-                sends.append((axis, 1))
-            if at <= 0 and -at < minus:
-                sends.append((axis, -1))
-        items.append((dict(offset), sends))
-        for axis, step in sends:
-            moved = dict(offset)
-            moved[axis] = moved.get(axis, 0) + step
-            visit(moved, order.index(axis))
-
-    visit({}, 0)
-    items.sort(key=lambda item: sum(abs(v) for v in item[0].values()))
-    return items
+def source(at, n, k):
+    both = jnp.minimum(at, n - 1 - at)
+    reach = (k + 1) // 2
+    paired = at - reach if k % 2 else at + reach
+    far = k - both
+    single = jnp.where(at + at < n - 1, at + far, at - far)
+    return jnp.where(k <= 2 * both, paired, single)
 
 
 def kernel(plan, rank_ref, lat_ref, ids_ref, w_ref, out_ref, xbuf, wbuf, lg, m_ref, s_ref, p_ref, stats, got,
@@ -78,7 +66,8 @@
     y, core = dp // 2, dp % 2
     z, x = vocab // nx, vocab % nx
     me = vocab * ny + y
-    half = lat_ref.shape[2] // 2
+    model = lat_ref.shape[2]
+    first_width = max(model // LANES // 7, 1) * LANES
     depth, cw = plan.depth, plan.cw
 
     def chip_device(b):
@@ -88,7 +77,7 @@
 
     base = pl.multiple_of(me * rows, rows)
     if rows != plan.per_dev:
-        xbuf[pl.ds(base, rows), :] = jnp.zeros((rows, 2 * half), jnp.bfloat16)
+        xbuf[pl.ds(base, rows), :] = jnp.zeros((rows, model), jnp.bfloat16)
     xbuf[pl.ds(base, plan.per_dev), :] = lat_ref[rank_ref[dp, 0]]
 
     barrier = pltpu.get_barrier_semaphore()
@@ -117,24 +106,48 @@
     pl.semaphore_wait(barrier, chips)
 
     def x_slice(flow, b):
-        return xbuf.at[pl.ds(pl.multiple_of(b * rows, rows), rows), pl.ds(flow * half, half)]
-
-    def origin(offset):
-        oy = lax.rem(y - offset.get("y", 0) + ny, ny)
-        ox = lax.rem(x - offset.get("x", 0) + nx, nx)
-        oz = lax.rem(z - offset.get("z", 0) + nz, nz)
-        return (oz * nx + ox) * ny + oy
-
-    def x_copy(flow, b, axis, step):
-        ty = lax.rem(y + (step if axis == "y" else 0) + ny, ny)
-        tx = lax.rem(x + (step if axis == "x" else 0) + nx, nx)
-        tz = lax.rem(z + (step if axis == "z" else 0) + nz, nz)
+        cols = pl.ds(0, first_width) if flow == 0 else pl.ds(first_width, model - first_width)
+        return xbuf.at[pl.ds(pl.multiple_of(b * rows, rows), plan.sent_rows), cols]
+
+    def chip(iy, ix, iz):
+        return (iz * nx + ix) * ny + iy
+
+    spot = {"y": (y, ny), "x": (x, nx), "z": (z, nz)}
+
+    sends = []
+
+    def x_copy(flow, b, axis, step, slot):
+        to = {name: at for name, (at, _) in spot.items()}
+        to[axis] = to[axis] + step
         return pltpu.make_async_remote_copy(
-            src_ref=x_slice(flow, b), dst_ref=x_slice(flow, b), send_sem=x_send, recv_sem=x_recv.at[flow, b],
-            device_id={"dp": ty * 2 + core, "vocab": tz * nx + tx}, device_id_type=MESH,
+            src_ref=x_slice(flow, b), dst_ref=x_slice(flow, b), send_sem=x_send.at[slot], recv_sem=x_recv.at[flow, b],
+            device_id={"dp": to["y"] * 2 + core, "vocab": to["z"] * nx + to["x"]}, device_id_type=MESH,
         )
 
-    flows = (flow_items(plan, ("y", "x", "z"), False), flow_items(plan, ("y", "z", "x"), True))
+    def send(flow, b, axis, step, here):
+        copy = x_copy(flow, b, axis, step, len(sends))
+        sends.append((copy, here))
+        if here is None:
+            copy.start()
+        else:
+            pl.when(here)(copy.start)
+
+    def spread(flow, b, axis):
+        at, n = spot[axis]
+        if n == 2:
+            send(flow, b, axis, 1 - 2 * at, None)
+        elif n > 2:
+            send(flow, b, axis, 1, at + 1 < n)
+            send(flow, b, axis, -1, at > 0)
+
+    def onward(flow, b, axis, origin):
+        at, n = spot[axis]
+        if n > 2:
+            step = jnp.where(origin < at, 1, -1)
+            send(flow, b, axis, step, jnp.logical_and(at + step >= 0, at + step < n))
+
+    def arrived(flow, b):
+        x_copy(flow, b, "y", 0, 0).wait_recv()
 
     def wy_copy(k, j):
         y_to = lax.rem(y + k, ny)
@@ -154,10 +167,9 @@
         )
 
     started = []
-    for flow in range(2):
-        offset, sends = flows[flow][0]
-        for axis, step in sends:
-            x_copy(flow, me, axis, step).start()
+    for axis in ("y", "x", "z"):
+        for flow in (1, 0):
+            spread(flow, me, axis)
     for j in range(plan.chunks):
         for k in range(1, ny):
             copy = wy_copy(k, j)
@@ -175,38 +187,69 @@
             copy.start()
             started.append(copy)
 
-    todo = [(flow, item) for pair in zip(flows[0][1:], flows[1][1:]) for flow, item in enumerate(pair)]
-    due = 0
-    for count, (flow, (offset, sends)) in enumerate(todo):
-        b = origin(offset)
-        x_copy(flow, b, "y", 0).wait_recv()
-        for axis, step in sends:
-            x_copy(flow, b, axis, step).start()
-        while due < plan.chunks - 1 and (count + 1) * (plan.chunks - 0.5) >= (due + 2) * len(todo):
-            forward_w(due)
-            due += 1
-
-    m_ref[...] = jnp.full(m_ref.shape, -jnp.inf, jnp.float32)
-    s_ref[...] = jnp.zeros(s_ref.shape, jnp.float32)
-    p_ref[...] = jnp.zeros(p_ref.shape, jnp.float32)
+    src = {
+        axis: [spot[axis][0]] + [source(*spot[axis], k) for k in range(1, spot[axis][1])] for axis in spot
+    }
+
+    def y_items():
+        for iy in src["y"][1:]:
+            for flow in (1, 0):
+                b = chip(iy, x, z)
+                arrived(flow, b)
+                onward(flow, b, "y", iy)
+                for axis in ("x", "z"):
+                    spread(flow, b, axis)
+
+    def first_x_items():
+        for ix in src["x"][1:]:
+            for iy in src["y"]:
+                b = chip(iy, ix, z)
+                arrived(0, b)
+                onward(0, b, "x", ix)
+                spread(0, b, "z")
+
+    def first_z_items(k):
+        iz = src["z"][k]
+        for ix in src["x"]:
+            for iy in src["y"]:
+                b = chip(iy, ix, iz)
+                arrived(0, b)
+                onward(0, b, "z", iz)
+
+    def second_z_items(k):
+        iz = src["z"][k]
+        for iy in src["y"]:
+            b = chip(iy, x, iz)
+            arrived(1, b)
+            onward(1, b, "z", iz)
+            spread(1, b, "x")
+
+    def second_x_items(k):
+        iz = src["z"][k]
+        for ix in src["x"][1:]:
+            for iy in src["y"]:
+                b = chip(iy, ix, iz)
+                arrived(1, b)
+                onward(1, b, "x", ix)
+
     lane = lax.broadcasted_iota(jnp.int32, (1, LANES), 1)
     repeated = y * plan.own_tiles * LANES - plan.start(y)
-    for j in range(plan.chunks):
-        while due < min(plan.chunks, j + 1):
-            forward_w(due)
-            due += 1
-        locals_[j].wait()
-        for k in range(ny):
-            wp_copy(k, j).wait_recv()
-
-        @pl.loop(0, plan.tokens // plan.m_tile)
-        def _(i, j=j):
-            top = pl.multiple_of(i * plan.m_tile, plan.m_tile)
+    m_tile = plan.m_tile
+
+    def score(k, low, high):
+        top = pl.multiple_of(src["z"][k] * m_tile, m_tile)
+
+        @pl.loop(low, high)
+        def _(j):
+            start = pl.multiple_of(j * cw, cw)
             lg[...] = jnp.dot(
-                xbuf[pl.ds(top, plan.m_tile), :], wbuf[:, w_cols(j)], preferred_element_type=jnp.float32
+                xbuf[pl.ds(top, m_tile), :], wbuf[:, pl.ds(start, cw)], preferred_element_type=jnp.float32
             )
-
-            @pl.loop(0, plan.m_tile // 32, unroll=2)
+            columns = [lane + (start + c * LANES) for c in range(cw // LANES)]
+            own = [at >= repeated for at in columns]
+            columns = [jnp.where(mine, at, -(2**30)) for mine, at in zip(own, columns)]
+
+            @pl.loop(0, m_tile // 32, unroll=2)
             def _(r):
                 here = pl.ds(pl.multiple_of(r * 32, 32), 32)
                 there = pl.ds(pl.multiple_of(top + r * 32, 32), 32)
@@ -219,19 +262,46 @@
                 picked = p_ref[there, :]
                 ids = ids_ref[there, :]
                 for c, part in enumerate(parts):
-                    first = j * cw + c * LANES
-                    columns = lane + first
-                    term = jnp.exp(part - now)
-                    match = columns == ids
-                    if first < (plan.own_tiles * ny - plan.tiles) * LANES:
-                        own = columns >= repeated
-                        term = jnp.where(own, term, 0.0)
-                        match = jnp.logical_and(match, own)
-                    total = total + term
-                    picked = picked + jnp.where(match, part, 0.0)
+                    total = total + jnp.where(own[c], jnp.exp(part - now), 0.0)
+                    picked = picked + jnp.where(columns[c] == ids, part, 0.0)
                 m_ref[there, :] = now
                 s_ref[there, :] = total
                 p_ref[there, :] = picked
+
+    def w_ready(j):
+        forward_w(j)
+        locals_[j].wait()
+        for k in range(ny):
+            wp_copy(k, j).wait_recv()
+
+    m_ref[...] = jnp.full(m_ref.shape, -jnp.inf, jnp.float32)
+    s_ref[...] = jnp.zeros(s_ref.shape, jnp.float32)
+    p_ref[...] = jnp.zeros(p_ref.shape, jnp.float32)
+    y_items()
+    first_x_items()
+    if nz > 1:
+        second_z_items(1)
+    second_x_items(0)
+    done_w = 0
+    for k in range(1, nz):
+        if k + 1 < nz:
+            second_z_items(k + 1)
+        first_z_items(k)
+        second_x_items(k)
+        if k == nz - 1:
+            break
+        until = plan.chunks * (k + 1) // nz
+        for j in range(done_w, until):
+            w_ready(j)
+        for t in range(k):
+            score(t, done_w, until)
+        score(k, 0, until)
+        done_w = until
+    for j in range(done_w, plan.chunks):
+        w_ready(j)
+    for t in range(nz - 1):
+        score(t, done_w, plan.chunks)
+    score(nz - 1, 0, plan.chunks)
 
     for g in range(plan.tokens // LANES):
         here = pl.ds(g * LANES, LANES)
@@ -258,8 +328,11 @@
     got[0] = stats[me // per_group]
     for copy in started:
         copy.wait_send()
-    sent = xbuf.at[pl.ds(0, (chips - 1) * rows), :]
-    pltpu.make_async_copy(sent, sent, x_send).wait()
+    for copy, here in sends:
+        if here is None:
+            copy.wait_send()
+        else:
+            pl.when(here)(copy.wait_send)
     others = got.at[pl.ds(1, chips - 1)]
     pltpu.make_async_copy(others, others, st_send).wait()
     pltpu.make_async_copy(others, others, st_recv).wait()
@@ -313,7 +386,7 @@
             vmem((plan.tokens, LANES), jnp.float32),
             vmem((plan.tokens // LANES, 8, LANES), jnp.float32),
             vmem((plan.chips, 8, LANES), jnp.float32),
-            dma, dma((2, plan.chips)),
+            dma((plan.x_sends(),)), dma((2, plan.chips)),
             dma((plan.chunks,)),
             dma((plan.ny, plan.chunks)), dma((plan.ny, plan.chunks)),
             dma((plan.ny, plan.chunks)), dma((plan.ny, plan.chunks)),

time: 131 us -> 106 us (0.81)
  Pallas kernels: 125 us -> 99.8 us
    pallas_call x1, Pallas kernels: 125 us -> 99.8 us  [per_device(): pl.pallas_call(functools.partial(kernel, plan), out_shape=jax.ShapeDtypeS...]
where the time goes in v2:
time: 106 us; the launch traced here: 105 us
  Pallas kernels  99.8 us (94%)
  local copies, waits for them, and re-layouts  4.76 us (4%)
    pallas_call x1, Pallas kernels, per_device(): pl.pallas_call(functools.partial(kernel, plan), out_shape=jax.ShapeDtypeS...  99.8 us
    unnamed x5, local copies, waits for them, and re-layouts  2.47 us

profile of v2, /device:TPU:0, one launch (start us, length us, event | category | flops | bytes accessed | tf_op | source)
XLA Modules:
  0.0 105.4 jit_solution(17799424253428361373)
XLA Ops:
  0.0 0.7 reshape.18
  0.8 0.1 squeeze.8
  0.8 0.1 squeeze.9
  0.9 0.7 compare_reduce_fusion
  1.6 0.1 broadcast_in_dim.10
  1.7 0.1 broadcast_select_fusion
  1.8 1.3 %reshape.20.ids_ref = s32[1024,1]{1,0:T(8,128)} reshape(s32[8,2,64]{2,1,0:T(2,128)S(1)} %pad.4.clone) | data formatting | bytes 8192 | tf_op jit(solution)/shard_map/reshape | solution.py:367
  3.1 1.4 %copy.10.rank_ref = s32[4,2]{1,0:T(4,128)} copy(s32[4,2]{0,1:T(2,128)} %param.6) | data formatting | bytes 64 | tf_op args[2]
  4.5 99.8 %score.1 = f32[1,56]{1,0:T(1,128)} custom-call(s32[4,2]{1,0:T(4,128)} %copy.10.rank_ref, bf16[2,56,3584]{2,1,0:T(8,128)(2,1)} %lat_ref.1, s32[1024,1]{1,0:T(8,128)} %reshape.20.ids_ref, bf16[896,2432]{1,0:T(8,128)(2,1)} %w_ref.1), custom_call_target="tpu_custom_call" | custom-call | tf_op jit(solution)/shard_map/score/pallas_call | solution.py:370
  104.3 1.1 %copy.16 = f32[1,56]{1,0:T(1,128)} copy(f32[1,56]{1,0:T(1,128)} %score.1) | data formatting | bytes 448
  (6 shorter events, 0.0 us)

commit v3 on v2

--- a/solution.py
+++ b/solution.py
@@ -286,10 +286,10 @@
     for k in range(1, nz):
         if k + 1 < nz:
             second_z_items(k + 1)
+        if k == nz - 1:
+            break
         first_z_items(k)
         second_x_items(k)
-        if k == nz - 1:
-            break
         until = plan.chunks * (k + 1) // nz
         for j in range(done_w, until):
             w_ready(j)
@@ -299,8 +299,11 @@
         done_w = until
     for j in range(done_w, plan.chunks):
         w_ready(j)
-    for t in range(nz - 1):
-        score(t, done_w, plan.chunks)
+        for t in range(nz - 1):
+            score(t, j, j + 1)
+    if nz > 1:
+        first_z_items(nz - 1)
+        second_x_items(nz - 1)
     score(nz - 1, 0, plan.chunks)
 
     for g in range(plan.tokens // LANES):

time: 106 us -> 107 us (level)
  Pallas kernels: 99.8 us -> 101 us
where the time goes in v3:
time: 107 us; the launch traced here: 106 us
  Pallas kernels  101 us (94%)
  local copies, waits for them, and re-layouts  4.76 us (4%)
    pallas_call x1, Pallas kernels, per_device(): pl.pallas_call(functools.partial(kernel, plan), out_shape=jax.ShapeDtypeS...  101 us
    unnamed x5, local copies, waits for them, and re-layouts  2.47 us

profile of v3, /device:TPU:0, one launch (start us, length us, event | category | flops | bytes accessed | tf_op | source)
XLA Modules:
  0.0 106.2 jit_solution(5497032218921829384)
XLA Ops:
  0.0 0.7 reshape.18
  0.8 0.1 squeeze.8
  0.8 0.1 squeeze.9
  0.9 0.7 compare_reduce_fusion
  1.6 0.1 broadcast_in_dim.10
  1.7 0.1 broadcast_select_fusion
  1.8 1.3 %reshape.20.ids_ref = s32[1024,1]{1,0:T(8,128)} reshape(s32[8,2,64]{2,1,0:T(2,128)S(1)} %pad.4.clone) | data formatting | bytes 8192 | tf_op jit(solution)/shard_map/reshape | solution.py:370
  3.1 1.4 %copy.10.rank_ref = s32[4,2]{1,0:T(4,128)} copy(s32[4,2]{0,1:T(2,128)} %param.6) | data formatting | bytes 64 | tf_op args[2]
  4.5 100.6 %score.1 = f32[1,56]{1,0:T(1,128)} custom-call(s32[4,2]{1,0:T(4,128)} %copy.10.rank_ref, bf16[2,56,3584]{2,1,0:T(8,128)(2,1)} %lat_ref.1, s32[1024,1]{1,0:T(8,128)} %reshape.20.ids_ref, bf16[896,2432]{1,0:T(8,128)(2,1)} %w_ref.1), custom_call_target="tpu_custom_call" | custom-call | tf_op jit(solution)/shard_map/score/pallas_call | solution.py:373
  105.1 1.1 %copy.16 = f32[1,56]{1,0:T(1,128)} copy(f32[1,56]{1,0:T(1,128)} %score.1) | data formatting | bytes 448
  (6 shorter events, 0.0 us)
